TPU v7x, 32 devices: a whole 2x2x4 slice. The times are simulated.
32 devices in a mesh: elem: 4 (over y, x), pulse: 8 (over z, core).
Axes of the slice: x: 2, y: 2, z: 4, core: 2. Of those that a mesh axis runs over, the one named last changes fastest.
Arguments:
- echoes: bfloat16 [2, 2048, 256, 256], P(None, 'elem', 'pulse'), may hold values from -6 to 6
- keep_mask: int32 [256, 8], P('pulse'), may hold values from 0 to 1, as said below
- steer_index: int32 [512], replicated, may hold values from 0 to 1023
- element_position: float32 [2048], replicated, may hold values from 0 to 1024
- element_gain: float32 [2, 2048], replicated, may hold values from -4 to 4
- steer_sines: float32 [1024], replicated, may hold values from -1 to 1
Outputs:
- doppler_power: float32 [512, 256, 256], P('pulse', None, 'elem')
Inputs may be any that keep to these rules, and one draw needn't show every extreme that they name: `keep_mask`: in each masking block, each aligned run of 32 pulses keeps at most 24 pulses, and at least one; in every masking block some run keeps exactly 24.
All inputs are finite; a program needn't handle non-finite values.
Results may differ from a plain program's by a relative error of at most 0.005.
Values may be sent and summed in bfloat16 or wider, within the bound.
No kernel may reach another device: no remote copies, remote signals or barrier semaphores. Data moves between devices by JAX's collectives and lax.ppermute only.
A program may use at most 128 MiB of HBM per device.

v0:
```python
import math
import jax
import jax.numpy as jnp
from jax import lax
from jax.sharding import PartitionSpec as P

E = 2048
P_SIZE = 256
RBLK = 32


def steering(element_position, element_gain, sines):
    phase = 2.0 * math.pi * element_position[:, None] * sines[None, :]
    cosine = jnp.cos(phase)
    sine = jnp.sin(phase)
    factor = 1.0 / math.sqrt(E)
    real = (element_gain[0][:, None] * cosine + element_gain[1][:, None] * sine) * factor
    imag = (element_gain[1][:, None] * cosine - element_gain[0][:, None] * sine) * factor
    return (real.astype(jnp.bfloat16), imag.astype(jnp.bfloat16))


def tables(count):
    index = jnp.arange(count, dtype=jnp.int32)
    angle = 2.0 * math.pi * (index[:, None] * index[None, :] % count).astype(jnp.float32) / count
    taper = 0.54 - 0.46 * jnp.cos(2.0 * math.pi * index.astype(jnp.float32) / (count - 1))
    taper = taper / math.sqrt(count)
    cos_table = jnp.cos(angle) * taper[None, :]
    sin_table = jnp.sin(angle) * taper[None, :]
    upper = jnp.concatenate((cos_table, sin_table), axis=1)
    lower = jnp.concatenate((-sin_table, cos_table), axis=1)
    transform = jnp.concatenate((upper, lower), axis=0)
    high = transform.astype(jnp.bfloat16)
    low = (transform - high.astype(jnp.float32)).astype(jnp.bfloat16)
    return (high, low)


def contract(left, right):
    return lax.dot_general(
        left, right, (((0,), (0,)), ((), ())), preferred_element_type=jnp.float32
    )


def per_device(echoes, keep_mask, steer_index, element_position, element_gain, steer_sines):
    choices_all = jnp.arange(steer_sines.shape[0], dtype=jnp.int32)
    sines = jnp.sum(
        jnp.where(steer_index[:, None] == choices_all[None, :], steer_sines[None, :], 0.0), axis=1
    )
    weight_re, weight_im = steering(element_position, element_gain, sines)
    high, low = tables(P_SIZE)
    count = P_SIZE
    groups = lax.axis_size("elem")
    local_elems = echoes.shape[1]
    local_pulses = echoes.shape[2]
    total_cells = echoes.shape[3]
    cells = total_cells // groups
    blocks_all = keep_mask.shape[1]
    kept_slots = (3 * local_pulses + 3) // 4
    offset = lax.axis_index("elem") * cells
    rank = jnp.cumsum(keep_mask, axis=0) - 1
    slot_ids = jnp.arange(kept_slots, dtype=jnp.int32)
    selector = (
        (keep_mask[None, :, :] == 1) & (rank[None, :, :] == slot_ids[:, None, None])
    ).astype(jnp.bfloat16)
    shaped5 = echoes.reshape(2, local_elems, local_pulses, blocks_all, total_cells // blocks_all)
    prepared = jnp.einsum("spk,cepkr->ceskr", selector, shaped5, preferred_element_type=jnp.float32)
    prepared = prepared.astype(jnp.bfloat16).reshape(2, local_elems, kept_slots, total_cells)
    turned = lax.all_to_all(prepared, "elem", split_axis=3, concat_axis=1, tiled=True)
    span = turned.shape[3]
    flat = turned.reshape(2, turned.shape[1], turned.shape[2] * span)
    real = contract(weight_re, flat[0]) - contract(weight_im, flat[1])
    imag = contract(weight_re, flat[1]) + contract(weight_im, flat[0])
    real = real.astype(jnp.bfloat16).reshape(-1, turned.shape[2], span)
    imag = imag.astype(jnp.bfloat16).reshape(-1, turned.shape[2], span)
    packed_re = real
    packed_im = imag
    block_ids = jnp.arange(blocks_all, dtype=jnp.int32)
    onehot = (
        (offset + jnp.arange(cells, dtype=jnp.int32))[:, None] // RBLK == block_ids[None, :]
    ).astype(jnp.bfloat16)
    spread = jnp.einsum("spk,nk->spn", selector, onehot, preferred_element_type=jnp.float32).astype(
        jnp.bfloat16
    )
    real = jnp.einsum("spn,bsn->bpn", spread, packed_re, preferred_element_type=jnp.float32).astype(
        jnp.bfloat16
    )
    imag = jnp.einsum("spn,bsn->bpn", spread, packed_im, preferred_element_type=jnp.float32).astype(
        jnp.bfloat16
    )
    beam_re = lax.all_to_all(real, "pulse", split_axis=0, concat_axis=1, tiled=True)
    beam_im = lax.all_to_all(imag, "pulse", split_axis=0, concat_axis=1, tiled=True)
    total = None
    for table in (high, low):
        part_re = jnp.einsum(
            "fp,bpn->bfn", table[:, :count], beam_re, preferred_element_type=jnp.float32
        )
        part_im = jnp.einsum(
            "fp,bpn->bfn", table[:, count:], beam_im, preferred_element_type=jnp.float32
        )
        total = part_re + part_im if total is None else total + part_re + part_im
    doppler_real = total[:, :count]
    doppler_imag = total[:, count:]
    return doppler_real * doppler_real + doppler_imag * doppler_imag


def solution(mesh):
    placed = (P(None, "elem", "pulse", None), P("pulse", None), P(), P(), P(), P())
    return jax.shard_map(
        per_device, mesh=mesh, in_specs=placed, out_specs=P("pulse", None, "elem"), check_vma=False
    )
```

profile of v0, /device:TPU:0, one launch (start us, length us, event | category | flops | bytes accessed | tf_op | source)
XLA Modules:
  0.0 494.8 jit_solution(7825158454604493364)
XLA Ops:
  0.0 0.7 broadcast_compare_fusion
  0.7 0.8 copy.85
  1.5 0.1 reduce_window_sum.11
  1.5 0.1 copy.86
  1.6 26.3 %copy.87 = bf16[2,512,32,256]{1,3,2,0:T(8,128)(2,1)} copy(bf16[2,512,32,256]{3,2,1,0:T(8,128)(2,1)} %param.6) | data formatting | bytes 33554432 | tf_op args[0]
  27.9 21.7 %convert_bitcast_fusion = bf16[2,512,24,8,32]{1,2,4,0,3:T(8,128)(2,1)} fusion(bf16[2,512,32,8,32]{1,4,3,2,0:T(8,128)(2,1)} %bitcast.62, pred[24,32,8,1,1]{1,2,0,4,3:T(8,128)(4,1)S(1)} %fusion.38), kind=kOutput, calls=%fused_computation.2 | convolution fusion | flops 408944640 | bytes 29366272 | tf_op jit(solution)/shard_map/spk,cepkr->ceskr/dot_general | solution.py:65
  49.6 9.4 %copy.90 = bf16[2,512,24,8,32]{1,4,3,2,0:T(8,128)(2,1)S(1)} copy(bf16[2,512,24,8,32]{1,2,4,0,3:T(8,128)(2,1)} %convert_bitcast_fusion) | data formatting | bytes 25165824 | tf_op jit(solution)/shard_map/convert_element_type | solution.py:66
  59.0 23.9 %copy.91 = bf16[2,512,24,256]{1,2,0,3:T(8,128)(2,1)} copy(bf16[2,512,24,256]{1,3,2,0:T(8,128)(2,1)S(1)} %bitcast.64) | data formatting | bytes 25165824 | tf_op jit(solution)/shard_map/reshape | solution.py:66
  83.0 6.4 %all-to-all-start = ((bf16[2,512,24,256]{1,2,0,3:T(8,128)(2,1)}), bf16[2,512,24,256]{1,2,0,3:T(8,128)(2,1)}, u32[]{:S(2)}, u32[]{:S(2)}) async-start(bf16[2,512,24,256]{1,2,0,3:T(8,128)(2,1)} %copy.91), calls=%async_computation | async-start | bytes 25165824 | tf_op jit(solution)/shard_map/all_to_all | solution.py:67
  89.4 0.3 convolution_convert_fusion
  89.7 0.3 copy.97
  90.0 0.4 select_reduce_fusion
  90.4 137.9 %all-to-all-done = bf16[2,512,24,256]{1,2,0,3:T(8,128)(2,1)} async-done(((bf16[2,512,24,256]{1,2,0,3:T(8,128)(2,1)}), bf16[2,512,24,256]{1,2,0,3:T(8,128)(2,1)}, u32[]{:S(2)}, u32[]{:S(2)}) %all-to-all-start) | async-done | bytes 12582944 | tf_op jit(solution)/shard_map/all_to_all | solution.py:67
  228.3 9.3 %copy.92 = bf16[2,512,24,256]{1,3,2,0:T(8,128)(2,1)S(1)} copy(bf16[2,512,24,256]{1,2,0,3:T(8,128)(2,1)} %all-to-all-done) | data formatting | bytes 25165824 | tf_op jit(solution)/shard_map/all_to_all | solution.py:67
  237.6 5.3 %fusion.49 = (bf16[1,4,512,24,64]{2,4,1,3,0:T(8,128)(2,1)}, bf16[1,4,512,24,64]{2,4,1,3,0:T(8,128)(2,1)}) fusion(bf16[2,4,512,24,64]{2,4,1,3,0:T(8,128)(2,1)S(1)} %bitcast.63), kind=kLoop, calls=%fused_computation.75 | loop fusion | bytes 25165824 | tf_op jit(solution)/shard_map/slice | solution.py:70
  242.9 8.5 %copy.94 = bf16[1,4,512,24,64]{2,1,4,3,0:T(4,128)(2,1)S(1)} copy(bf16[1,4,512,24,64]{2,4,1,3,0:T(8,128)(2,1)} %get-tuple-element.5) | data formatting | bytes 12582912 | tf_op jit(solution)/shard_map/slice | solution.py:70
  251.4 5.3 %copy.117 = bf16[192,8,4,512]{3,1,2,0:T(8,128)(2,1)} copy(bf16[192,8,4,512]{3,2,1,0:T(4,128)(2,1)S(1)} %bitcast.69) | data formatting | bytes 12582912
  256.8 8.7 %copy.93 = bf16[1,4,512,24,64]{2,1,4,3,0:T(4,128)(2,1)S(1)} copy(bf16[1,4,512,24,64]{2,4,1,3,0:T(8,128)(2,1)} %get-tuple-element.6) | data formatting | bytes 12582912 | tf_op jit(solution)/shard_map/slice | solution.py:70
  265.4 0.0 slice-start
  265.4 2.7 copy.116
  268.2 0.0 slice-start.1
  268.2 18.6 %fusion.21 = f32[512,1536]{1,0:T(8,128)S(1)} fusion(bf16[2048,1536]{0,1:T(8,128)(2,1)S(1)} %bitcast.73, f32[2048]{0:T(1024)S(1)} %bitcast.85, f32[512]{0:T(512)S(1)} %select_reduce_fusion, f32[2048]{0:T(1024)S(1)} %broadcast_multiply_fusion, f32[2048]{0:T(1024)S(1)} %bitcast.81), kind=kOutput, calls=%fused_computation.28 | convolution fusion | flops 3227516928 | bytes 9463808 | tf_op jit(solution)/shard_map/dot_general | solution.py:38
  286.9 18.3 %fusion.15 = bf16[512,1536]{1,0:T(8,128)(2,1)S(1)} fusion(f32[512,1536]{1,0:T(8,128)S(1)} %fusion.21, bf16[2048,1536]{0,1:T(8,128)(2,1)S(1)} %bitcast.78, f32[2048]{0:T(1024)S(1)} %bitcast.86, f32[512]{0:T(512)S(1)} %select_reduce_fusion, f32[2048]{0:T(1024)S(1)} %broadcast_multiply_fusion, f32[2048]{0:T(1024)S(1)} %bitcast.82), kind=kOutput, calls=%fused_computation.21 | convolution fusion | flops 3229089792 | bytes 11036672 | tf_op jit(solution)/shard_map/dot_general | solution.py:38
  305.2 1.6 copy.95
  306.8 2.8 convert_bitcast_fusion.2
  309.6 7.8 %copy.98 = bf16[512,32,64]{2,1,0:T(8,128)(2,1)} copy(bf16[512,32,64]{0,1,2:T(8,128)(2,1)S(1)} %convert_bitcast_fusion.2) | data formatting | bytes 4194304 | tf_op jit(solution)/shard_map/convert_element_type | solution.py:83
  317.4 7.6 %reshape.90 = bf16[8,2,65536]{2,1,0:T(2,128)(2,1)} reshape(bf16[512,32,64]{2,1,0:T(8,128)(2,1)} %copy.98) | data formatting | bytes 4194304
  325.0 5.2 %all-to-all-start.1 = ((bf16[8,2,65536]{2,1,0:T(2,128)(2,1)}), bf16[8,2,65536]{2,1,0:T(2,128)(2,1)S(1)}, u32[]{:S(2)}, u32[]{:S(2)}) async-start(bf16[8,2,65536]{2,1,0:T(2,128)(2,1)} %reshape.90), calls=%async_computation.1 | async-start | bytes 4194304 | tf_op jit(solution)/shard_map/all_to_all | solution.py:89
  330.2 21.1 %fusion.19 = f32[512,1536]{1,0:T(8,128)S(1)} fusion(bf16[2048,1536]{0,1:T(8,128)(2,1)} %bitcast.75, f32[2048]{0:T(1024)S(1)} %bitcast.87, f32[512]{0:T(512)S(1)} %select_reduce_fusion, f32[2048]{0:T(1024)S(1)} %broadcast_multiply_fusion, f32[2048]{0:T(1024)S(1)} %bitcast.83), kind=kOutput, calls=%fused_computation.27 | convolution fusion | flops 3227516928 | bytes 9463808 | tf_op jit(solution)/shard_map/dot_general | solution.py:38
  351.4 22.4 %fusion.16 = bf16[512,1536]{1,0:T(8,128)(2,1)} fusion(f32[512,1536]{1,0:T(8,128)S(1)} %fusion.19, bf16[2048,1536]{0,1:T(8,128)(2,1)} %bitcast.74, f32[2048]{0:T(1024)S(1)} %bitcast.88, f32[512]{0:T(512)S(1)} %select_reduce_fusion, f32[2048]{0:T(1024)S(1)} %broadcast_multiply_fusion, f32[2048]{0:T(1024)S(1)} %bitcast.84), kind=kOutput, calls=%fused_computation.22 | convolution fusion | flops 3229089792 | bytes 11036672 | tf_op jit(solution)/shard_map/dot_general | solution.py:38
  373.7 2.6 copy.101
  376.3 4.1 convert_bitcast_fusion.1
  380.5 8.8 %copy.104 = bf16[512,32,64]{2,1,0:T(8,128)(2,1)} copy(bf16[512,32,64]{0,1,2:T(8,128)(2,1)} %convert_bitcast_fusion.1) | data formatting | bytes 4194304 | tf_op jit(solution)/shard_map/convert_element_type | solution.py:86
  389.2 7.6 %reshape.92 = bf16[8,2,65536]{2,1,0:T(2,128)(2,1)} reshape(bf16[512,32,64]{2,1,0:T(8,128)(2,1)} %copy.104) | data formatting | bytes 4194304
  396.8 0.0 all-to-all-done.1
  396.8 5.1 %all-to-all-start.2 = ((bf16[8,2,65536]{2,1,0:T(2,128)(2,1)}), bf16[8,2,65536]{2,1,0:T(2,128)(2,1)}, u32[]{:S(2)}, u32[]{:S(2)}) async-start(bf16[8,2,65536]{2,1,0:T(2,128)(2,1)} %reshape.92), calls=%async_computation.2 | async-start | bytes 4194304 | tf_op jit(solution)/shard_map/all_to_all | solution.py:90
  401.9 1.1 sine_multiply_fusion
  403.0 0.1 subtract_convert_fusion
  403.1 5.0 %reshape.91 = bf16[512,32,64]{2,1,0:T(8,128)(2,1)} reshape(bf16[8,2,65536]{2,1,0:T(2,128)(2,1)S(1)} %all-to-all-done.1) | data formatting | bytes 4194304
  408.1 5.4 %copy.99 = bf16[8,64,32,64]{3,2,0,1:T(8,128)(2,1)} copy(bf16[8,64,32,64]{3,2,1,0:T(8,128)(2,1)} %bitcast.71) | data formatting | bytes 4194304 | tf_op jit(solution)/shard_map/all_to_all | solution.py:89
  413.5 37.5 %all-to-all-done.2 = bf16[8,2,65536]{2,1,0:T(2,128)(2,1)} async-done(((bf16[8,2,65536]{2,1,0:T(2,128)(2,1)}), bf16[8,2,65536]{2,1,0:T(2,128)(2,1)}, u32[]{:S(2)}, u32[]{:S(2)}) %all-to-all-start.2) | async-done | bytes 2097184 | tf_op jit(solution)/shard_map/all_to_all | solution.py:90
  451.0 7.6 %reshape.93 = bf16[512,32,64]{2,1,0:T(8,128)(2,1)} reshape(bf16[8,2,65536]{2,1,0:T(2,128)(2,1)} %all-to-all-done.2) | data formatting | bytes 4194304
  458.6 3.3 copy.105
  462.0 2.4 fusion.30
  464.4 5.6 %fusion.31 = f32[64,64,512]{2,1,0:T(8,128)} fusion(bf16[64,256,64]{2,1,0:T(8,128)(2,1)S(1)} %bitcast.65, bf16[512,512]{1,0:T(8,128)(2,1)S(1)} %fusion.25), kind=kOutput, calls=%fused_computation.47 | convolution fusion | flops 1073741824 | bytes 12845056 | tf_op jit(solution)/shard_map/fp,bpn->bfn/dot_general | solution.py:93
  470.0 5.6 %fusion.29 = f32[64,64,512]{2,1,0:T(8,128)} fusion(bf16[64,256,64]{2,1,0:T(8,128)(2,1)S(1)} %bitcast.66, bf16[512,512]{1,0:T(8,128)(2,1)S(1)} %subtract_convert_fusion), kind=kOutput, calls=%fused_computation.43 | convolution fusion | flops 1073741824 | bytes 12845056 | tf_op jit(solution)/shard_map/fp,bpn->bfn/dot_general | solution.py:93
  475.7 12.0 %add_bitcast_fusion = f32[64,512,64]{1,2,0:T(8,128)} fusion(f32[64,64,512]{2,1,0:T(8,128)} %fusion.29, f32[64,64,512]{2,1,0:T(8,128)} %fusion.31, f32[64,64,512]{2,1,0:T(8,128)S(1)} %fusion.30, bf16[64,256,64]{2,1,0:T(8,128)(2,1)S(1)} %bitcast.68, bf16[512,512]{1,0:T(8,128)(2,1)S(1)} %subtract_convert_fusion), kind=kOutput, calls=%fused_computation.3 | convolution fusion | flops 1080033280 | bytes 38010880 | tf_op jit(solution)/shard_map/fp,bpn->bfn/dot_general | solution.py:96
  487.7 6.7 %fusion.14 = f32[64,256,64]{1,2,0:T(8,128)} fusion(f32[64,512,64]{1,2,0:T(8,128)} %add_bitcast_fusion), kind=kLoop, calls=%fused_computation.17 | loop fusion | flops 3145728 | bytes 12582912 | tf_op jit(solution)/shard_map/add | solution.py:102
  (22 shorter events, 0.2 us)
Async XLA Ops:
  83.0 7.1 %copy-start.4 = (f32[1024]{0:T(1024)S(1)}, f32[1024]{0:T(1024)}, u32[]{:S(2)}) copy-start(f32[1024]{0:T(1024)} %param.11) | copy-start | bytes 12292
  83.0 7.1 %copy-start.5 = (s32[512]{0:T(512)S(1)}, s32[512]{0:T(512)}, u32[]{:S(2)}) copy-start(s32[512]{0:T(512)} %param.8) | copy-start | bytes 6148
  83.0 7.4 %copy-start.3 = (f32[2048]{0:T(1024)S(1)}, f32[2048]{0:T(1024)}, u32[]{:S(2)}) copy-start(f32[2048]{0:T(1024)} %param.9) | copy-start | bytes 24580
  83.0 7.4 %copy-start.2 = (f32[2,2048]{1,0:T(2,128)S(1)}, f32[2,2048]{1,0:T(2,128)}, u32[]{:S(2)}) copy-start(f32[2,2048]{1,0:T(2,128)} %param.10) | copy-start | bytes 49156
  83.0 145.3 %all-to-all-start = ((bf16[2,512,24,256]{1,2,0,3:T(8,128)(2,1)}), bf16[2,512,24,256]{1,2,0,3:T(8,128)(2,1)}, u32[]{:S(2)}, u32[]{:S(2)}) async-start(bf16[2,512,24,256]{1,2,0,3:T(8,128)(2,1)} %copy.91), calls=%async_computation | async-start | bytes 25165824 | tf_op jit(solution)/shard_map/all_to_all | solution.py:67
  265.4 21.4 %slice-start = ((s8[6291456]{0:T(1024)(128)(4,1)}), s8[4194304]{0:T(1024)(128)(4,1)S(1)}, s32[]{:S(2)}) async-start(s8[6291456]{0:T(1024)(128)(4,1)} %bitcast.76), calls=%async_computation.3 | async-start | bytes 8388608
  268.2 18.7 %copy-start.1 = (bf16[192,8,4,512]{3,1,2,0:T(8,128)(2,1)}, bf16[192,8,4,512]{3,1,2,0:T(8,128)(2,1)S(1)}, u32[]{:S(2)}) copy-start(bf16[192,8,4,512]{3,1,2,0:T(8,128)(2,1)S(1)} %copy.116) | copy-start | bytes 18874372
  268.2 18.7 %slice-start.1 = ((s8[6291456]{0:T(1024)(128)(4,1)}), s8[2097152]{0:T(1024)(128)(4,1)S(1)}, s32[]{:S(2)}) async-start(s8[6291456]{0:T(1024)(128)(4,1)} %bitcast.76), calls=%async_computation.4 | async-start | bytes 4194304
  325.0 71.8 %all-to-all-start.1 = ((bf16[8,2,65536]{2,1,0:T(2,128)(2,1)}), bf16[8,2,65536]{2,1,0:T(2,128)(2,1)S(1)}, u32[]{:S(2)}, u32[]{:S(2)}) async-start(bf16[8,2,65536]{2,1,0:T(2,128)(2,1)} %reshape.90), calls=%async_computation.1 | async-start | bytes 4194304 | tf_op jit(solution)/shard_map/all_to_all | solution.py:89
  396.8 54.2 %all-to-all-start.2 = ((bf16[8,2,65536]{2,1,0:T(2,128)(2,1)}), bf16[8,2,65536]{2,1,0:T(2,128)(2,1)}, u32[]{:S(2)}, u32[]{:S(2)}) async-start(bf16[8,2,65536]{2,1,0:T(2,128)(2,1)} %reshape.92), calls=%async_computation.2 | async-start | bytes 4194304 | tf_op jit(solution)/shard_map/all_to_all | solution.py:90
  462.0 2.4 copy-start
where the time goes:
time: 503 us; the launch traced here: 495 us
  waiting for transfers between devices  175 us (35%)
  local copies, waits for them, and re-layouts  158 us (31%)
  matrix products  135 us (27%)
  starting transfers between devices  16.8 us (3%)
  other arithmetic  9.09 us (2%)
    all_to_all x1, waiting for transfers between devices, per_device(): lax.all_to_all(prepared, 'elem', split_axis=3, concat_axis=1, tiled=True)  138 us
    dot_general x4, matrix products, contract(): lax.dot_general(left, right, (((0,), (0,)), ((), ())), preferred_element_...  80.4 us
    unnamed x24, local copies, waits for them, and re-layouts  62.8 us
    all_to_all x1, waiting for transfers between devices, per_device(): lax.all_to_all(imag, 'pulse', split_axis=0, concat_axis=1, tiled=True)  37.5 us
    reshape x1, local copies, waits for them, and re-layouts, per_device(): prepared.astype(jnp.bfloat16)  23.9 us
    slice x3, local copies, waits for them, and re-layouts, per_device(): real = contract(weight_re, flat[0]) - contract(weight_im, flat[1])  22.5 us
    dot_general x1, matrix products, per_device(): jnp.einsum('spk,cepkr->ceskr', selector, shaped5, preferred_element_type=...  21.7 us
    dot_general x2, matrix products, per_device(): jnp.einsum('fp,bpn->bfn', table[:, count:], beam_im, preferred_element_ty...  14.4 us
  transfers between devices with their start and end apart: 3, of which 2 were waited for; matrix products, arithmetic and copies ran while one was open for 16% of the time, Pallas kernels for 0%

commit v1 on v0

--- a/solution.py
+++ b/solution.py
@@ -64,7 +64,9 @@
     shaped5 = echoes.reshape(2, local_elems, local_pulses, blocks_all, total_cells // blocks_all)
     prepared = jnp.einsum("spk,cepkr->ceskr", selector, shaped5, preferred_element_type=jnp.float32)
     prepared = prepared.astype(jnp.bfloat16).reshape(2, local_elems, kept_slots, total_cells)
-    turned = lax.all_to_all(prepared, "elem", split_axis=3, concat_axis=1, tiled=True)
+    shards = jnp.split(prepared, lax.axis_size("elem"), axis=3)
+    received = lax.all_to_all(jnp.stack(shards), "elem", 0, 0)
+    turned = jnp.concatenate(received, axis=1)
     span = turned.shape[3]
     flat = turned.reshape(2, turned.shape[1], turned.shape[2] * span)
     real = contract(weight_re, flat[0]) - contract(weight_im, flat[1])

time: 503 us -> 484 us (0.962)
  local copies, waits for them, and re-layouts: 158 us -> 132 us
  other arithmetic: 9.09 us -> 14.7 us
    reshape x1 -> x0, local copies, waits for them, and re-layouts: 23.9 us -> none  [per_device(): prepared.astype(jnp.bfloat16)]
    all_to_all x1 -> x0, local copies, waits for them, and re-layouts: 9.3 us -> none  [per_device(): lax.all_to_all(prepared, 'elem', split_axis=3, concat_axis=1, tiled=True)]
    another operation x0 -> x1, other arithmetic: none -> 5.6 us  [per_device(): received = lax.all_to_all(jnp.stack(shards), 'elem', 0, 0)]
    slice x3, local copies, waits for them, and re-layouts: 22.5 us -> 27.9 us  [per_device(): real = contract(weight_re, flat[0]) - contract(weight_im, flat[1])]
  transfers between devices with their start and end apart: 3 -> 3, of which waited for: 2 -> 2; matrix products, arithmetic and copies ran while one was open for 16% -> 17% of each run, Pallas kernels for 0% -> 0%
where the time goes in v1:
time: 484 us; the launch traced here: 474 us
  waiting for transfers between devices  175 us (36%)
  matrix products  135 us (28%)
  local copies, waits for them, and re-layouts  132 us (27%)
  starting transfers between devices  17 us (4%)
  other arithmetic  14.7 us (3%)
    all_to_all x1, waiting for transfers between devices, per_device(): received = lax.all_to_all(jnp.stack(shards), 'elem', 0, 0)  138 us
    dot_general x4, matrix products, contract(): lax.dot_general(left, right, (((0,), (0,)), ((), ())), preferred_element_...  80.5 us
    unnamed x24, local copies, waits for them, and re-layouts  62.8 us
    all_to_all x1, waiting for transfers between devices, per_device(): lax.all_to_all(imag, 'pulse', split_axis=0, concat_axis=1, tiled=True)  37.5 us
    slice x3, local copies, waits for them, and re-layouts, per_device(): real = contract(weight_re, flat[0]) - contract(weight_im, flat[1])  27.9 us
    dot_general x1, matrix products, per_device(): jnp.einsum('spk,cepkr->ceskr', selector, shaped5, preferred_element_type=...  21.7 us
    dot_general x2, matrix products, per_device(): jnp.einsum('fp,bpn->bfn', table[:, count:], beam_im, preferred_element_ty...  14.4 us
    dot_general x2, matrix products, per_device(): jnp.einsum('fp,bpn->bfn', table[:, :count], beam_re, preferred_element_ty...  11.3 us
  transfers between devices with their start and end apart: 3, of which 2 were waited for; matrix products, arithmetic and copies ran while one was open for 17% of the time, Pallas kernels for 0%

profile of v1, /device:TPU:0, one launch (start us, length us, event | category | flops | bytes accessed | tf_op | source)
XLA Modules:
  0.0 474.2 jit_solution(3742169964461354859)
XLA Ops:
  0.0 0.7 broadcast_compare_fusion
  0.7 0.8 copy.81
  1.5 0.1 reduce_window_sum.11
  1.5 0.1 copy.82
  1.6 26.3 %copy.83 = bf16[2,512,32,256]{1,3,2,0:T(8,128)(2,1)} copy(bf16[2,512,32,256]{3,2,1,0:T(8,128)(2,1)} %param.6) | data formatting | bytes 33554432 | tf_op args[0]
  27.9 21.7 %convert_bitcast_fusion = bf16[2,512,24,8,32]{1,2,4,0,3:T(8,128)(2,1)} fusion(bf16[2,512,32,8,32]{1,4,3,2,0:T(8,128)(2,1)} %bitcast.68, pred[24,32,8,1,1]{1,2,0,4,3:T(8,128)(4,1)S(1)} %fusion.38), kind=kOutput, calls=%fused_computation.3 | convolution fusion | flops 408944640 | bytes 29366272 | tf_op jit(solution)/shard_map/spk,cepkr->ceskr/dot_general | solution.py:65
  49.6 9.4 %copy.86 = bf16[2,512,24,8,32]{1,4,3,2,0:T(8,128)(2,1)S(1)} copy(bf16[2,512,24,8,32]{1,2,4,0,3:T(8,128)(2,1)} %convert_bitcast_fusion) | data formatting | bytes 25165824 | tf_op jit(solution)/shard_map/convert_element_type | solution.py:66
  59.0 1.6 slice_bitcast_fusion.3
  60.7 5.6 %pad_maximum_fusion = bf16[4,2,512,24,64]{2,4,3,1,0:T(8,128)(2,1)} fusion(bf16[1,2,512,24,64]{2,4,3,1,0:T(8,128)(2,1)S(1)} %get-tuple-element.8, bf16[1,2,512,24,64]{2,4,3,1,0:T(8,128)(2,1)S(1)} %get-tuple-element.9, bf16[1,2,512,24,64]{2,4,3,1,0:T(8,128)(2,1)S(1)} %get-tuple-element.10, bf16[1,2,512,24,64]{2,4,3,1,0:T(8,128)(2,1)S(1)} %get-tuple-element.7), kind=kLoop, calls=%fused_computation.2 | loop fusion | flops 18874368 | bytes 25165824 | tf_op jit(solution)/shard_map/stack | solution.py:68
  66.3 6.4 %all-to-all-start = ((bf16[4,2,512,24,64]{2,4,3,1,0:T(8,128)(2,1)}), bf16[4,2,512,24,64]{2,4,3,1,0:T(8,128)(2,1)}, u32[]{:S(2)}, u32[]{:S(2)}) async-start(bf16[4,2,512,24,64]{2,4,3,1,0:T(8,128)(2,1)} %pad_maximum_fusion), calls=%async_computation | async-start | bytes 25165824 | tf_op jit(solution)/shard_map/all_to_all | solution.py:68
  72.8 0.3 convolution_convert_fusion
  73.1 0.3 copy.91
  73.4 0.4 select_reduce_fusion
  73.8 137.9 %all-to-all-done = bf16[4,2,512,24,64]{2,4,3,1,0:T(8,128)(2,1)} async-done(((bf16[4,2,512,24,64]{2,4,3,1,0:T(8,128)(2,1)}), bf16[4,2,512,24,64]{2,4,3,1,0:T(8,128)(2,1)}, u32[]{:S(2)}, u32[]{:S(2)}) %all-to-all-start) | async-done | bytes 12582944 | tf_op jit(solution)/shard_map/all_to_all | solution.py:68
  211.6 10.7 %fusion.49 = (bf16[1,4,512,24,64]{2,4,3,0,1:T(8,128)(2,1)}, bf16[1,4,512,24,64]{2,4,3,0,1:T(8,128)(2,1)}) fusion(bf16[2,4,512,24,64]{2,4,3,0,1:T(8,128)(2,1)} %bitcast.10), kind=kLoop, calls=%fused_computation.80 | loop fusion | bytes 25165824 | tf_op jit(solution)/shard_map/slice | solution.py:72
  222.3 8.5 %copy.88 = bf16[1,4,512,24,64]{2,1,4,3,0:T(4,128)(2,1)S(1)} copy(bf16[1,4,512,24,64]{2,4,3,0,1:T(8,128)(2,1)} %get-tuple-element.5) | data formatting | bytes 12582912 | tf_op jit(solution)/shard_map/slice | solution.py:72
  230.8 5.3 %copy.111 = bf16[192,8,4,512]{3,1,2,0:T(8,128)(2,1)} copy(bf16[192,8,4,512]{3,2,1,0:T(4,128)(2,1)S(1)} %bitcast.74) | data formatting | bytes 12582912
  236.2 8.7 %copy.87 = bf16[1,4,512,24,64]{2,1,4,3,0:T(4,128)(2,1)S(1)} copy(bf16[1,4,512,24,64]{2,4,3,0,1:T(8,128)(2,1)} %get-tuple-element.6) | data formatting | bytes 12582912 | tf_op jit(solution)/shard_map/slice | solution.py:72
  244.9 0.0 slice-start
  244.9 2.7 copy.110
  247.7 0.0 slice-start.1
  247.7 18.6 %fusion.21 = f32[512,1536]{1,0:T(8,128)S(1)} fusion(bf16[2048,1536]{0,1:T(8,128)(2,1)S(1)} %bitcast.78, f32[2048]{0:T(1024)S(1)} %bitcast.90, f32[512]{0:T(512)S(1)} %select_reduce_fusion, f32[2048]{0:T(1024)S(1)} %broadcast_multiply_fusion, f32[2048]{0:T(1024)S(1)} %bitcast.86), kind=kOutput, calls=%fused_computation.33 | convolution fusion | flops 3227516928 | bytes 9463808 | tf_op jit(solution)/shard_map/dot_general | solution.py:38
  266.3 18.3 %fusion.15 = bf16[512,1536]{1,0:T(8,128)(2,1)S(1)} fusion(f32[512,1536]{1,0:T(8,128)S(1)} %fusion.21, bf16[2048,1536]{0,1:T(8,128)(2,1)S(1)} %bitcast.83, f32[2048]{0:T(1024)S(1)} %bitcast.91, f32[512]{0:T(512)S(1)} %select_reduce_fusion, f32[2048]{0:T(1024)S(1)} %broadcast_multiply_fusion, f32[2048]{0:T(1024)S(1)} %bitcast.87), kind=kOutput, calls=%fused_computation.26 | convolution fusion | flops 3229089792 | bytes 11036672 | tf_op jit(solution)/shard_map/dot_general | solution.py:38
  284.6 1.6 copy.89
  286.2 2.8 convert_bitcast_fusion.2
  289.0 7.8 %copy.92 = bf16[512,32,64]{2,1,0:T(8,128)(2,1)} copy(bf16[512,32,64]{0,1,2:T(8,128)(2,1)S(1)} %convert_bitcast_fusion.2) | data formatting | bytes 4194304 | tf_op jit(solution)/shard_map/convert_element_type | solution.py:85
  296.8 7.6 %reshape.92 = bf16[8,2,65536]{2,1,0:T(2,128)(2,1)} reshape(bf16[512,32,64]{2,1,0:T(8,128)(2,1)} %copy.92) | data formatting | bytes 4194304
  304.4 5.4 %all-to-all-start.1 = ((bf16[8,2,65536]{2,1,0:T(2,128)(2,1)}), bf16[8,2,65536]{2,1,0:T(2,128)(2,1)S(1)}, u32[]{:S(2)}, u32[]{:S(2)}) async-start(bf16[8,2,65536]{2,1,0:T(2,128)(2,1)} %reshape.92), calls=%async_computation.1 | async-start | bytes 4194304 | tf_op jit(solution)/shard_map/all_to_all | solution.py:91
  309.8 20.9 %fusion.19 = f32[512,1536]{1,0:T(8,128)S(1)} fusion(bf16[2048,1536]{0,1:T(8,128)(2,1)} %bitcast.80, f32[2048]{0:T(1024)S(1)} %bitcast.92, f32[512]{0:T(512)S(1)} %select_reduce_fusion, f32[2048]{0:T(1024)S(1)} %broadcast_multiply_fusion, f32[2048]{0:T(1024)S(1)} %bitcast.88), kind=kOutput, calls=%fused_computation.32 | convolution fusion | flops 3227516928 | bytes 9463808 | tf_op jit(solution)/shard_map/dot_general | solution.py:38
  330.8 22.6 %fusion.16 = bf16[512,1536]{1,0:T(8,128)(2,1)} fusion(f32[512,1536]{1,0:T(8,128)S(1)} %fusion.19, bf16[2048,1536]{0,1:T(8,128)(2,1)} %bitcast.79, f32[2048]{0:T(1024)S(1)} %bitcast.93, f32[512]{0:T(512)S(1)} %select_reduce_fusion, f32[2048]{0:T(1024)S(1)} %broadcast_multiply_fusion, f32[2048]{0:T(1024)S(1)} %bitcast.89), kind=kOutput, calls=%fused_computation.27 | convolution fusion | flops 3229089792 | bytes 11036672 | tf_op jit(solution)/shard_map/dot_general | solution.py:38
  353.4 2.6 copy.95
  356.0 4.2 convert_bitcast_fusion.1
  360.1 8.8 %copy.98 = bf16[512,32,64]{2,1,0:T(8,128)(2,1)} copy(bf16[512,32,64]{0,1,2:T(8,128)(2,1)} %convert_bitcast_fusion.1) | data formatting | bytes 4194304 | tf_op jit(solution)/shard_map/convert_element_type | solution.py:88
  368.9 7.6 %reshape.94 = bf16[8,2,65536]{2,1,0:T(2,128)(2,1)} reshape(bf16[512,32,64]{2,1,0:T(8,128)(2,1)} %copy.98) | data formatting | bytes 4194304
  376.5 0.0 all-to-all-done.1
  376.5 5.1 %all-to-all-start.2 = ((bf16[8,2,65536]{2,1,0:T(2,128)(2,1)}), bf16[8,2,65536]{2,1,0:T(2,128)(2,1)}, u32[]{:S(2)}, u32[]{:S(2)}) async-start(bf16[8,2,65536]{2,1,0:T(2,128)(2,1)} %reshape.94), calls=%async_computation.2 | async-start | bytes 4194304 | tf_op jit(solution)/shard_map/all_to_all | solution.py:92
  381.6 1.1 sine_multiply_fusion
  382.7 0.1 subtract_convert_fusion
  382.8 5.0 %reshape.93 = bf16[512,32,64]{2,1,0:T(8,128)(2,1)} reshape(bf16[8,2,65536]{2,1,0:T(2,128)(2,1)S(1)} %all-to-all-done.1) | data formatting | bytes 4194304
  387.8 5.4 %copy.93 = bf16[8,64,32,64]{3,2,0,1:T(8,128)(2,1)} copy(bf16[8,64,32,64]{3,2,1,0:T(8,128)(2,1)} %bitcast.76) | data formatting | bytes 4194304 | tf_op jit(solution)/shard_map/all_to_all | solution.py:91
  393.2 37.5 %all-to-all-done.2 = bf16[8,2,65536]{2,1,0:T(2,128)(2,1)} async-done(((bf16[8,2,65536]{2,1,0:T(2,128)(2,1)}), bf16[8,2,65536]{2,1,0:T(2,128)(2,1)}, u32[]{:S(2)}, u32[]{:S(2)}) %all-to-all-start.2) | async-done | bytes 2097184 | tf_op jit(solution)/shard_map/all_to_all | solution.py:92
  430.7 7.5 %reshape.95 = bf16[512,32,64]{2,1,0:T(8,128)(2,1)} reshape(bf16[8,2,65536]{2,1,0:T(2,128)(2,1)} %all-to-all-done.2) | data formatting | bytes 4194304
  438.3 3.3 copy.99
  441.6 2.4 fusion.30
  444.0 5.6 %fusion.31 = f32[64,64,512]{2,1,0:T(8,128)} fusion(bf16[64,256,64]{2,1,0:T(8,128)(2,1)S(1)} %bitcast.70, bf16[512,512]{1,0:T(8,128)(2,1)S(1)} %fusion.25), kind=kOutput, calls=%fused_computation.52 | convolution fusion | flops 1073741824 | bytes 12845056 | tf_op jit(solution)/shard_map/fp,bpn->bfn/dot_general | solution.py:95
  449.6 5.6 %fusion.29 = f32[64,64,512]{2,1,0:T(8,128)} fusion(bf16[64,256,64]{2,1,0:T(8,128)(2,1)S(1)} %bitcast.71, bf16[512,512]{1,0:T(8,128)(2,1)S(1)} %subtract_convert_fusion), kind=kOutput, calls=%fused_computation.48 | convolution fusion | flops 1073741824 | bytes 12845056 | tf_op jit(solution)/shard_map/fp,bpn->bfn/dot_general | solution.py:95
  455.3 12.0 %add_bitcast_fusion = f32[64,512,64]{1,2,0:T(8,128)} fusion(f32[64,64,512]{2,1,0:T(8,128)} %fusion.29, f32[64,64,512]{2,1,0:T(8,128)} %fusion.31, f32[64,64,512]{2,1,0:T(8,128)S(1)} %fusion.30, bf16[64,256,64]{2,1,0:T(8,128)(2,1)S(1)} %bitcast.73, bf16[512,512]{1,0:T(8,128)(2,1)S(1)} %subtract_convert_fusion), kind=kOutput, calls=%fused_computation.4 | convolution fusion | flops 1080033280 | bytes 38010880 | tf_op jit(solution)/shard_map/fp,bpn->bfn/dot_general | solution.py:98
  467.3 6.7 %fusion.14 = f32[64,256,64]{1,2,0:T(8,128)} fusion(f32[64,512,64]{1,2,0:T(8,128)} %add_bitcast_fusion), kind=kLoop, calls=%fused_computation.18 | loop fusion | flops 3145728 | bytes 12582912 | tf_op jit(solution)/shard_map/add | solution.py:104
  (22 shorter events, 0.2 us)
Async XLA Ops:
  66.3 7.1 %copy-start.4 = (f32[1024]{0:T(1024)S(1)}, f32[1024]{0:T(1024)}, u32[]{:S(2)}) copy-start(f32[1024]{0:T(1024)} %param.11) | copy-start | bytes 12292
  66.3 7.1 %copy-start.5 = (s32[512]{0:T(512)S(1)}, s32[512]{0:T(512)}, u32[]{:S(2)}) copy-start(s32[512]{0:T(512)} %param.8) | copy-start | bytes 6148
  66.3 7.4 %copy-start.3 = (f32[2048]{0:T(1024)S(1)}, f32[2048]{0:T(1024)}, u32[]{:S(2)}) copy-start(f32[2048]{0:T(1024)} %param.9) | copy-start | bytes 24580
  66.3 7.4 %copy-start.2 = (f32[2,2048]{1,0:T(2,128)S(1)}, f32[2,2048]{1,0:T(2,128)}, u32[]{:S(2)}) copy-start(f32[2,2048]{1,0:T(2,128)} %param.10) | copy-start | bytes 49156
  66.3 145.3 %all-to-all-start = ((bf16[4,2,512,24,64]{2,4,3,1,0:T(8,128)(2,1)}), bf16[4,2,512,24,64]{2,4,3,1,0:T(8,128)(2,1)}, u32[]{:S(2)}, u32[]{:S(2)}) async-start(bf16[4,2,512,24,64]{2,4,3,1,0:T(8,128)(2,1)} %pad_maximum_fusion), calls=%async_computation | async-start | bytes 25165824 | tf_op jit(solution)/shard_map/all_to_all | solution.py:68
  244.9 21.4 %slice-start = ((s8[6291456]{0:T(1024)(128)(4,1)}), s8[4194304]{0:T(1024)(128)(4,1)S(1)}, s32[]{:S(2)}) async-start(s8[6291456]{0:T(1024)(128)(4,1)} %bitcast.81), calls=%async_computation.3 | async-start | bytes 8388608
  247.7 18.6 %copy-start.1 = (bf16[192,8,4,512]{3,1,2,0:T(8,128)(2,1)}, bf16[192,8,4,512]{3,1,2,0:T(8,128)(2,1)S(1)}, u32[]{:S(2)}) copy-start(bf16[192,8,4,512]{3,1,2,0:T(8,128)(2,1)S(1)} %copy.110) | copy-start | bytes 18874372
  247.7 18.6 %slice-start.1 = ((s8[6291456]{0:T(1024)(128)(4,1)}), s8[2097152]{0:T(1024)(128)(4,1)S(1)}, s32[]{:S(2)}) async-start(s8[6291456]{0:T(1024)(128)(4,1)} %bitcast.81), calls=%async_computation.4 | async-start | bytes 4194304
  304.4 72.0 %all-to-all-start.1 = ((bf16[8,2,65536]{2,1,0:T(2,128)(2,1)}), bf16[8,2,65536]{2,1,0:T(2,128)(2,1)S(1)}, u32[]{:S(2)}, u32[]{:S(2)}) async-start(bf16[8,2,65536]{2,1,0:T(2,128)(2,1)} %reshape.92), calls=%async_computation.1 | async-start | bytes 4194304 | tf_op jit(solution)/shard_map/all_to_all | solution.py:91
  376.5 54.2 %all-to-all-start.2 = ((bf16[8,2,65536]{2,1,0:T(2,128)(2,1)}), bf16[8,2,65536]{2,1,0:T(2,128)(2,1)}, u32[]{:S(2)}, u32[]{:S(2)}) async-start(bf16[8,2,65536]{2,1,0:T(2,128)(2,1)} %reshape.94), calls=%async_computation.2 | async-start | bytes 4194304 | tf_op jit(solution)/shard_map/all_to_all | solution.py:92
  441.6 2.4 copy-start
